TPU v7x, 32 devices: a 4x4x1 block of a 4x4x8 slice. The times are simulated.
32 devices in a mesh: dp: 1 (over z), cols: 4 (over y), rows: 8 (over x, core).
Axes of the slice: x: 4, y: 4, z: 1, core: 2. Of those that a mesh axis runs over, the one named last changes fastest.
The devices are a block of a 4x4x8 slice.
Arguments:
- frames: bfloat16 [32, 1, 512, 256, 4], P(None, 'dp', 'rows', 'cols')
- w_in: bfloat16 [3, 3, 4, 256], replicated
- w_rec: bfloat16 [3, 3, 64, 256], replicated
- gate_bias: float32 [256], replicated
- h_init: bfloat16 [1, 512, 256, 64], P('dp', 'rows', 'cols')
- c_init: float32 [1, 512, 256, 64], P('dp', 'rows', 'cols')
Outputs:
- output 1: bfloat16 [32, 1, 512, 256, 64], P(None, 'dp', 'rows', 'cols')
- output 2: float32 [1, 512, 256, 64], P('dp', 'rows', 'cols')
All inputs are finite; a program needn't handle non-finite values.
Results may differ from a plain program's by a relative error of at most 0.00442392.
Values are sent between devices in bfloat16 or wider.
A program may use at most 768 MiB of HBM per device.

v0:
```python
import jax
import jax.numpy as jnp
from jax import lax
from jax.sharding import PartitionSpec as P, NamedSharding

CONV_DIMS = ("NHWC", "HWIO", "NHWC")


def conv_valid(operand, kernel):
    return lax.conv_general_dilated(operand, kernel, (1, 1), "VALID", dimension_numbers=CONV_DIMS, preferred_element_type=jnp.float32)


def cell_update(gate_pre, c_prev):
    gate_i, gate_f, gate_o, gate_g = jnp.split(gate_pre, 4, axis=-1)
    c_next = jax.nn.sigmoid(gate_f) * c_prev + jax.nn.sigmoid(gate_i) * jnp.tanh(gate_g)
    h_next = (jax.nn.sigmoid(gate_o) * jnp.tanh(c_next)).astype(jnp.bfloat16)
    return h_next, c_next


def edge_exchange(tile_in, axis_name, axis_size, axis_dim, width):
    length = tile_in.shape[axis_dim]
    low_part = lax.slice_in_dim(tile_in, 0, width, axis=axis_dim)
    high_part = lax.slice_in_dim(tile_in, length - width, length, axis=axis_dim)
    if axis_size == 1:
        from_prev = jnp.zeros_like(high_part)
        from_next = jnp.zeros_like(low_part)
    else:
        forward = [(source, source + 1) for source in range(axis_size - 1)]
        backward = [(source + 1, source) for source in range(axis_size - 1)]
        from_prev = lax.ppermute(high_part, axis_name, forward)
        from_next = lax.ppermute(low_part, axis_name, backward)
    return jnp.concatenate([from_prev, tile_in, from_next], axis=axis_dim)


def add_halo(tile_in, width, n_rows, n_cols):
    row_dim = tile_in.ndim - 3
    tall_tile = edge_exchange(tile_in, "rows", n_rows, row_dim, width)
    return edge_exchange(tall_tile, "cols", n_cols, row_dim + 1, width)


def solution(mesh):
    n_rows = mesh.shape["rows"]
    n_cols = mesh.shape["cols"]
    seq_spec = P(None, "dp", "rows", "cols", None)
    state_spec = P("dp", "rows", "cols", None)

    def local_run(frames, w_in, w_rec, gate_bias, h_init, c_init):
        frames_ext = add_halo(frames, 1, n_rows, n_cols)

        def time_step(carry_in, frame_ext):
            h_prev, c_prev = carry_in
            h_ext = add_halo(h_prev, 1, n_rows, n_cols)
            gate_pre = conv_valid(frame_ext, w_in) + conv_valid(h_ext, w_rec) + gate_bias
            h_next, c_next = cell_update(gate_pre, c_prev)
            return (h_next, c_next), h_next

        (h_last, c_last), hidden_seq = lax.scan(time_step, (h_init, c_init), frames_ext)
        return hidden_seq, c_last

    return jax.shard_map(local_run, mesh=mesh, in_specs=(seq_spec, P(), P(), P(), state_spec, state_spec), out_specs=(seq_spec, state_spec), check_vma=False)
```

profile of v0, /device:TPU:97, one launch (start us, length us, event | category | flops | bytes accessed | tf_op | source)
XLA Modules:
  0.0 1146.5 jit_solution(16296369228929143890)
XLA Ops:
  1.5 4.6 collective-permute-start.4
  8.0 4.9 copy.62
  29.0 6.2 pad_maximum_fusion.3
  35.2 1107.2 %while.14 = (s32[]{:T(128)}, bf16[1,64,64,64]{3,1,2,0:T(8,128)(2,1)S(1)}, f32[1,64,64,64]{3,1,2,0:T(8,128)}, bf16[32,1,64,64,64]{4,3,2,1,0:T(8,128)(2,1)}, bf16[...) while((s32[]{:T(128)}, ...), condition=%wide.region_1.2_spmd, body=%wide.region_0.1_spmd.sunk | while | flops 1457813632 | bytes 54611188 | solution.py:57
  47.5 5.1 collective-permute-start.3
  59.0 4.4 add_add_fusion.2
  93.9 4.4 add_add_fusion.2
  128.5 4.4 add_add_fusion.2
  163.0 4.4 add_add_fusion.2
  197.5 4.4 add_add_fusion.2
  232.1 4.4 add_add_fusion.2
  266.6 4.4 add_add_fusion.2
  301.1 4.4 add_add_fusion.2
  335.7 4.4 add_add_fusion.2
  370.2 4.4 add_add_fusion.2
  404.7 4.4 add_add_fusion.2
  439.3 4.4 add_add_fusion.2
  473.9 4.4 add_add_fusion.2
  508.4 4.4 add_add_fusion.2
  543.0 4.4 add_add_fusion.2
  577.5 4.4 add_add_fusion.2
  612.0 4.4 add_add_fusion.2
  715.7 4.4 add_add_fusion.2
  784.7 4.4 add_add_fusion.2
  819.2 4.4 add_add_fusion.2
  853.8 4.4 add_add_fusion.2
  888.4 4.4 add_add_fusion.2
  922.9 4.4 add_add_fusion.2
  957.4 4.4 add_add_fusion.2
  992.0 4.4 add_add_fusion.2
  1026.5 4.4 add_add_fusion.2
  1130.2 4.4 add_add_fusion.2
  (1281 shorter events, 999.0 us)
Async XLA Ops:
  1.5 11.5 %collective-permute-start.4 = (bf16[32,1,1,64,4]{3,0,4,2,1:T(8,128)(2,1)S(1)}, bf16[32,1,1,64,4]{3,0,4,2,1:T(8,128)(2,1)S(1)}, u32[]{:S(2)}, u32[]{:S(2)}) collective-permute-start(bf16[32,1,1,64,4]{3,0,4,2,1:T(8,128)(2,1)S(1)} %copy.70), channel_id=1, source_target_pairs={{0,1},{1,2},{2,3},{3,4},{4,5},{5,6},{6,7},{8,9},{9,10},{10,11},{11... | collective-permute-start | bytes 49160 | tf_op jit(solution)/shard_map/ppermute | solution.py:30
  6.1 9.5 collective-permute-start.5
  19.2 9.8 collective-permute-start.6
  36.1 9.3 collective-permute-start
  46.1 10.2 collective-permute-start.2
  81.6 9.5 collective-permute-start.2
  116.5 9.2 collective-permute-start.2
  151.1 9.2 collective-permute-start.2
  185.6 9.2 collective-permute-start.2
  220.1 9.2 collective-permute-start.2
  289.2 9.2 collective-permute-start.2
  323.7 9.2 collective-permute-start.2
  358.3 9.2 collective-permute-start.2
  392.8 9.2 collective-permute-start.2
  427.3 9.2 collective-permute-start.2
  461.9 9.2 collective-permute-start.2
  496.5 9.2 collective-permute-start.2
  531.0 9.2 collective-permute-start.2
  565.6 9.2 collective-permute-start.2
  600.1 9.2 collective-permute-start.2
  703.7 9.2 collective-permute-start.2
  772.8 9.2 collective-permute-start.2
  807.3 9.2 collective-permute-start.2
  841.8 9.2 collective-permute-start.2
  876.4 9.2 collective-permute-start.2
  910.9 9.2 collective-permute-start.2
  945.5 9.2 collective-permute-start.2
  980.0 9.2 collective-permute-start.2
  1014.6 9.2 collective-permute-start.2
  1049.1 9.2 collective-permute-start.2
  1083.7 9.2 collective-permute-start.2
  1118.2 9.2 collective-permute-start.2
  (266 other events, 1175.7 us)
where the time goes:
time: 1150 us
  starting transfers between devices  368 us (32%)
  local copies, waits for them, and re-layouts  356 us (31%)
  matrix products  258 us (22%)
  other arithmetic  156 us (14%)
    conv_general_dilated x64, matrix products, conv_valid(): lax.conv_general_dilated(operand, kernel, (1, 1), 'VALID', dimension_numb...  258 us
    ppermute x66, starting transfers between devices, edge_exchange(): from_prev = lax.ppermute(high_part, axis_name, forward)  257 us
    ppermute x66, starting transfers between devices, edge_exchange(): from_next = lax.ppermute(low_part, axis_name, backward)  112 us
    div x32, other arithmetic, cell_update(): jax.nn.sigmoid(gate_f) * c_prev + jax.nn.sigmoid(gate_i) * jnp.tanh(gate_g)  72.1 us
    conv_general_dilated x128, local copies, waits for them, and re-layouts, conv_valid(): lax.conv_general_dilated(operand, kernel, (1, 1), 'VALID', dimension_numb...  63 us
    while x320, local copies, waits for them, and re-layouts  58.1 us
    dynamic_update_slice x32, local copies, waits for them, and re-layouts, local_run(): lax.scan(time_step, (h_init, c_init), frames_ext)  54.1 us
    another operation x64, local copies, waits for them, and re-layouts  42.8 us
  transfers between devices with their start and end apart: 132, of which 0 were waited for; matrix products, arithmetic and copies ran while one was open for 19% of the time, Pallas kernels for 0%

commit v1 on v0

v1 whole, which is shorter than its diff:
```python
import functools

import jax
import jax.numpy as jnp
from jax import lax
from jax.experimental import pallas as pl
from jax.experimental.pallas import tpu as pltpu
from jax.sharding import PartitionSpec as P

MESH = pl.DeviceIdType.MESH
BF16, F32 = jnp.bfloat16, jnp.float32
LANES = 128


def chunk_order(n):
    order = [0]
    low, high = 1, n - 1
    while low <= high:
        order.append(low)
        if high != low:
            order.append(high)
        low, high = low + 1, high - 1
    return order


def cell_kernel(cfg, fr_ref, w_ref, bias_ref, h0_ref, c0_ref, mask_ref, out_ref, c_ref,
                ha, hb, left_a, left_b, right_a, right_b, gates,
                col_out, col_in, row_out, row_in, diag_in,
                col_ssem, col_rsem, row_ssem, row_rsem, diag_ssem, diag_rsem, out_sem):
    steps, half, chan, n_chunks, n_rows, n_cols = cfg
    per = half // n_chunks
    groups = chan // 16
    order = chunk_order(n_chunks)
    first, last = 0, n_chunks - 1
    my_row, my_col = lax.axis_index("rows"), lax.axis_index("cols")
    has_up, has_down = my_row > 0, my_row < n_rows - 1
    has_left, has_right = my_col > 0, my_col < n_cols - 1
    h_refs, l_refs, r_refs = (ha, hb), (left_a, left_b), (right_a, right_b)

    def mask(index):
        return mask_ref[index] > 0

    even, low_half = mask(0), mask(1)
    lane_first, lane_last = mask(2), mask(3)

    def copy(src, dst, ssem, rsem, drow, dcol):
        return pltpu.make_async_remote_copy(src_ref=src, dst_ref=dst, send_sem=ssem, recv_sem=rsem,
                                            device_id={"rows": my_row + drow, "cols": my_col + dcol}, device_id_type=MESH)

    def col_copy(par, side, chunk):
        return copy(col_out.at[par, side, chunk], col_in.at[par, side, chunk], col_ssem.at[par, side, chunk],
                    col_rsem.at[par, side, chunk], 0, 1 if side == 0 else -1)

    def row_copy(par, side):
        return copy(row_out.at[par, side], row_in.at[par, side], row_ssem.at[par, side], row_rsem.at[par, side],
                    1 if side == 0 else -1, 0)

    def diag_copy(par, slot):
        chunk = last if slot < 2 else first
        return copy(col_out.at[par, slot % 2, chunk], diag_in.at[par, slot], diag_ssem.at[par, slot],
                    diag_rsem.at[par, slot], 1 if slot < 2 else -1, 1 if slot % 2 == 0 else -1)

    col_to, col_from = (has_right, has_left), (has_left, has_right)
    row_to, row_from = (has_down, has_up), (has_up, has_down)
    diag_to = tuple((has_down if s < 2 else has_up) & col_to[s % 2] for s in range(4))
    diag_from = tuple((has_up if s < 2 else has_down) & col_from[s % 2] for s in range(4))

    def start_chunk(par, chunk, live):
        for side in range(2):
            @pl.when(col_to[side] & live)
            def _():
                col_copy(par, side, chunk).start()
        if chunk in (first, last):
            side = 0 if chunk == last else 1

            @pl.when(row_to[side] & live)
            def _():
                row_copy(par, side).start()
            for slot in ((0, 1) if chunk == last else (2, 3)):
                @pl.when(diag_to[slot] & live)
                def _():
                    diag_copy(par, slot).start()

    def wait_for(par, chunks, edge):
        for side in range(2):
            if chunks:
                @pl.when(col_from[side])
                def _():
                    for chunk in chunks:
                        col_copy(par, side, chunk).wait_recv()
                        col_copy(par, 1 - side, chunk).wait_send()
        if edge is not None:
            side = 0 if edge == first else 1

            @pl.when(row_from[side])
            def _():
                row_copy(par, side).wait_recv()
                row_copy(par, 1 - side).wait_send()
            for slot in ((0, 1) if edge == first else (2, 3)):
                @pl.when(diag_from[slot])
                def _():
                    diag_copy(par, slot).wait_recv()
                    diag_copy(par, 3 - slot).wait_send()

    def shifted(par, row, message, rolls):
        for g in range(groups):
            place = pl.ds(row * chan + 16 * g, 16)
            cells = h_refs[par][place, :]
            halo = pltpu.roll(message, rolls[g] % LANES, 1)
            l_refs[par][place, :] = jnp.where(lane_first, halo, pltpu.roll(cells, 1, 1))
            r_refs[par][place, :] = jnp.where(lane_last, halo, pltpu.roll(cells, LANES - 1, 1))

    def col_message(par, chunk):
        return jnp.where(even, col_in[par, 0, chunk], col_in[par, 1, chunk])

    def patch(par, chunks, edge):
        for chunk in chunks:
            message = col_message(par, chunk)
            for q in range(per):
                shifted(par, chunk * per + q + 1, message, [-2 * (q * groups + g) for g in range(groups)])
        if edge is not None:
            side = 0 if edge == first else 1
            diag = jnp.where(even, diag_in[par, 2 * side], diag_in[par, 2 * side + 1])
            other = last if edge == first else first
            q = per - 1 if edge == first else 0
            row = 0 if edge == first else half + 1
            for g in range(groups):
                place = slice(16 * g, 16 * (g + 1))
                mine, theirs = row_out[par, side, place, :], row_in[par, side, place, :]
                joined = jnp.where(low_half, theirs, mine) if edge == first else jnp.where(low_half, mine, theirs)
                h_refs[par][pl.ds(row * chan + 16 * g, 16), :] = joined
            message = jnp.where(mask(4 + side), diag, col_message(par, other))
            shifted(par, row, message, [64 - 2 * (q * groups + g) for g in range(groups)])

    def publish(par, chunk):
        parts = [h_refs[par][pl.ds((chunk * per + s // groups + 1) * chan + 16 * (s % groups), 16), :]
                 for s in range(per * groups)]
        level = 0
        while len(parts) > 1:
            keep = mask(6 + level)
            parts = [jnp.where(keep, parts[2 * i], pltpu.roll(parts[2 * i + 1], 2 << level, 1)) for i in range(len(parts) // 2)]
            level += 1
        col_out[par, 0, chunk] = pltpu.roll(parts[0], 65, 1)
        col_out[par, 1, chunk] = pltpu.roll(parts[0], 63, 1)
        if chunk in (first, last):
            side = 0 if chunk == last else 1
            row = half if chunk == last else 1
            for g in range(groups):
                row_out[par, side, 16 * g:16 * (g + 1), :] = pltpu.roll(h_refs[par][pl.ds(row * chan + 16 * g, 16), :], 64, 1)

    def multiply(par, t, chunk, slot):
        blocks = []
        for q in range(per):
            place = pl.ds((chunk * per + q) * chan, 3 * chan)
            frame = fr_ref[t, pl.ds((chunk * per + q) * 16, 48), :]
            blocks.append(jnp.concatenate([l_refs[par][place, :], h_refs[par][place, :], r_refs[par][place, :], frame], axis=0))
        gates[slot] = jnp.dot(w_ref[...], jnp.concatenate(blocks, axis=1), preferred_element_type=F32)

    def sigmoid(x):
        return 0.5 * jnp.tanh(0.5 * x) + 0.5

    def update(par, chunk, slot):
        for q in range(per):
            pre = [gates[slot, pl.ds(b * chan, chan), q * LANES:(q + 1) * LANES] + bias_ref[pl.ds(b * chan, chan), :]
                   for b in range(4)]
            place = pl.ds((chunk * per + q) * chan, chan)
            c_next = sigmoid(pre[1]) * c_ref[place, :] + sigmoid(pre[0]) * jnp.tanh(pre[3])
            c_ref[place, :] = c_next
            h_refs[par][pl.ds((chunk * per + q + 1) * chan, chan), :] = (sigmoid(pre[2]) * jnp.tanh(c_next)).astype(BF16)

    def out_copy(par, t):
        return pltpu.make_async_copy(h_refs[par].at[pl.ds(chan, half * chan), :], out_ref.at[t], out_sem.at[par])

    needs, seen = [], set()
    for chunk in order:
        chunks, edge = [], None
        for near in (chunk - 1, chunk, chunk + 1):
            if 0 <= near < n_chunks and near not in seen:
                seen.add(near)
                chunks.append(near)
        if chunk in (first, last):
            edge = chunk
        needs.append((chunks, edge))
    waits, waited = [], set()
    for chunks, edge in needs:
        group = list(chunks)
        if edge is not None:
            group.append(last if edge == first else first)
        group = [c for c in group if c not in waited]
        waited.update(group)
        waits.append((group, edge))

    for par in range(2):
        col_in[par] = jnp.zeros(col_in.shape[1:], BF16)
        row_in[par] = jnp.zeros(row_in.shape[1:], BF16)
        diag_in[par] = jnp.zeros(diag_in.shape[1:], BF16)
    barrier = pltpu.get_barrier_semaphore()
    count = jnp.int32(0)
    for drow in (-1, 0, 1):
        for dcol in (-1, 0, 1):
            if (drow, dcol) == (0, 0):
                continue
            there = jnp.bool_(True)
            if drow:
                there = there & (has_down if drow > 0 else has_up)
            if dcol:
                there = there & (has_right if dcol > 0 else has_left)

            @pl.when(there)
            def _():
                pl.semaphore_signal(barrier, inc=1, device_id={"rows": my_row + drow, "cols": my_col + dcol}, device_id_type=MESH)
            count = count + there.astype(jnp.int32)
    pl.semaphore_wait(barrier, count)

    c_ref[...] = c0_ref[...]
    ha[pl.ds(chan, half * chan), :] = h0_ref[...]
    for chunk in order:
        publish(0, chunk)
        start_chunk(0, chunk, True)

    def step(t, par, old):
        live = t < steps - 1

        @pl.when(old)
        def _():
            out_copy(1 - par, t - 2).wait()
        wait_for(par, *waits[0])
        patch(par, *needs[0])
        for i, chunk in enumerate(order):
            if i + 1 < n_chunks:
                wait_for(par, *waits[i + 1])
            multiply(par, t, chunk, i % 2)
            if i + 1 < n_chunks:
                patch(par, *needs[i + 1])
            if i > 0:
                update(1 - par, order[i - 1], (i - 1) % 2)
                publish(1 - par, order[i - 1])
                start_chunk(1 - par, order[i - 1], live)
        update(1 - par, order[-1], (n_chunks - 1) % 2)
        publish(1 - par, order[-1])
        start_chunk(1 - par, order[-1], live)
        out_copy(1 - par, t).start()

    def two_steps(i, carry):
        step(2 * i, 0, i > 0)
        step(2 * i + 1, 1, i > 0)
        return carry

    lax.fori_loop(0, steps // 2, two_steps, 0)
    out_copy(1, steps - 2).wait()
    out_copy(0, steps - 1).wait()


def lane_masks(per, groups):
    lane = jnp.arange(LANES)
    slots = per * groups
    corner = jnp.isin(lane, jnp.array([0, 63, 64, 127]))
    top = (2 * ((per - 1) * groups + jnp.arange(groups)))
    low = 2 * jnp.arange(groups)
    rows = [lane % 2 == 0, lane < 64, lane % 64 == 0, lane % 64 == 63,
            jnp.isin(lane, jnp.concatenate([top + 64, (top - 1) % LANES])),
            jnp.isin(lane, jnp.concatenate([low, low + 63]))]
    keep = corner
    level = 0
    while (1 << level) < slots:
        rows.append(keep)
        keep = keep | jnp.roll(keep, 2 << level)
        level += 1
    return jnp.broadcast_to(jnp.stack(rows)[:, None, :], (len(rows), 16, LANES)).astype(BF16)


def untile_kernel(x_ref, o_ref):
    half, chan = o_ref.shape[1] // 2, o_ref.shape[3]
    for k in range(half):
        cells = x_ref[0, pl.ds(k * chan, chan), :].T
        o_ref[0, k] = cells[:64]
        o_ref[0, k + half] = cells[64:]


def edge_exchange(tile_in, axis_name, axis_size, axis_dim):
    length = tile_in.shape[axis_dim]
    low_part = lax.slice_in_dim(tile_in, 0, 1, axis=axis_dim)
    high_part = lax.slice_in_dim(tile_in, length - 1, length, axis=axis_dim)
    if axis_size == 1:
        from_prev, from_next = jnp.zeros_like(high_part), jnp.zeros_like(low_part)
    else:
        forward = [(source, source + 1) for source in range(axis_size - 1)]
        backward = [(source + 1, source) for source in range(axis_size - 1)]
        from_prev = lax.ppermute(high_part, axis_name, forward)
        from_next = lax.ppermute(low_part, axis_name, backward)
    return jnp.concatenate([from_prev, tile_in, from_next], axis=axis_dim)


N_CHUNKS = 8


def solution(mesh):
    n_rows, n_cols = mesh.shape["rows"], mesh.shape["cols"]
    seq_spec = P(None, "dp", "rows", "cols", None)
    state_spec = P("dp", "rows", "cols", None)

    def local_run(frames, w_in, w_rec, gate_bias, h_init, c_init):
        steps, batch, height, width, c_in = frames.shape
        chan = h_init.shape[-1]
        half = height // 2
        assert batch == 1 and width == 64 and chan == 64 and c_in == 4 and steps % 2 == 0
        per, groups = half // N_CHUNKS, chan // 16

        def to_lanes(state):
            parts = state[0].reshape(2, half, width, chan).transpose(1, 3, 0, 2)
            return parts.reshape(half * chan, 2 * width)

        flat = frames[:, 0].transpose(0, 1, 3, 2)
        flat = edge_exchange(flat, "rows", n_rows, 1)
        flat = edge_exchange(flat, "cols", n_cols, 3)
        flat = jnp.stack([flat[..., dx:dx + width] for dx in range(3)], axis=2).reshape(steps, height + 2, 3 * c_in, width)
        flat = jnp.pad(flat, ((0, 0), (0, 0), (0, 16 - 3 * c_in), (0, 0)))
        flat = jnp.concatenate([flat[:, :half + 2], flat[:, half:]], axis=3).reshape(steps, (half + 2) * 16, LANES)

        gates_n = w_rec.shape[-1]
        w_h = w_rec.transpose(1, 0, 2, 3).reshape(9 * chan, gates_n)
        w_x = jnp.pad(w_in.reshape(3, 3 * c_in, gates_n), ((0, 0), (0, 16 - 3 * c_in), (0, 0))).reshape(48, gates_n)
        weights = jnp.concatenate([w_h, w_x], axis=0).T
        bias = jnp.broadcast_to(gate_bias[:, None], (gates_n, LANES))

        vmem = pl.BlockSpec(memory_space=pltpu.VMEM)
        cells = pltpu.VMEM(((half + 2) * chan, LANES), BF16)
        dma = pltpu.SemaphoreType.DMA
        cfg = (steps, half, chan, N_CHUNKS, n_rows, n_cols)
        hidden, c_last = pl.pallas_call(
            functools.partial(cell_kernel, cfg),
            out_shape=(jax.ShapeDtypeStruct((steps, half * chan, LANES), BF16), jax.ShapeDtypeStruct((half * chan, LANES), F32)),
            in_specs=[vmem] * 6,
            out_specs=(pl.BlockSpec(memory_space=pl.ANY), vmem),
            scratch_shapes=[cells] * 6 + [
                pltpu.VMEM((2, gates_n, per * LANES), F32),
                pltpu.VMEM((2, 2, N_CHUNKS, 16, LANES), BF16), pltpu.VMEM((2, 2, N_CHUNKS, 16, LANES), BF16),
                pltpu.VMEM((2, 2, chan, LANES), BF16), pltpu.VMEM((2, 2, chan, LANES), BF16),
                pltpu.VMEM((2, 4, 16, LANES), BF16),
                dma((2, 2, N_CHUNKS)), dma((2, 2, N_CHUNKS)), dma((2, 2)), dma((2, 2)), dma((2, 4)), dma((2, 4)), dma((2,)),
            ],
            compiler_params=pltpu.CompilerParams(collective_id=0, has_side_effects=True, vmem_limit_bytes=40 * 1024 * 1024),
        )(flat, weights, bias, to_lanes(h_init), to_lanes(c_init), lane_masks(per, groups))

        hidden_seq = pl.pallas_call(
            untile_kernel,
            out_shape=jax.ShapeDtypeStruct((steps, height, width, chan), BF16),
            grid=(steps,),
            in_specs=[pl.BlockSpec((1, half * chan, LANES), lambda t: (t, 0, 0))],
            out_specs=pl.BlockSpec((1, height, width, chan), lambda t: (t, 0, 0, 0)),
        )(hidden)
        c_last = c_last.reshape(half, chan, 2, width).transpose(2, 0, 3, 1).reshape(1, height, width, chan)
        return hidden_seq[:, None], c_last

    return jax.shard_map(local_run, mesh=mesh, in_specs=(seq_spec, P(), P(), P(), state_spec, state_spec),
                         out_specs=(seq_spec, state_spec), check_vma=False)
```

time: 1150 us -> 292 us (0.25)
  starting transfers between devices: 368 us -> 11.8 us
  local copies, waits for them, and re-layouts: 356 us -> 57.7 us
  matrix products: 258 us -> 0 us
  Pallas kernels: 0 us -> 196 us
  other arithmetic: 156 us -> 21.9 us
    conv_general_dilated x64 -> x0, matrix products: 258 us -> none  [conv_valid(): lax.conv_general_dilated(operand, kernel, (1, 1), 'VALID', dimension_numb...]
    ppermute x66 -> x2, starting transfers between devices: 257 us -> 8.38 us  [edge_exchange(): from_prev = lax.ppermute(high_part, axis_name, forward)]
    pallas_call x0 -> x2, Pallas kernels: none -> 196 us  [the longest x1 165 us: local_run(): pl.pallas_call(functools.partial(cell_kernel, cfg), out_shape=(jax.ShapeD...]
    ppermute x66 -> x2, starting transfers between devices: 112 us -> 3.43 us  [edge_exchange(): from_next = lax.ppermute(low_part, axis_name, backward)]
    div x32 -> x0, other arithmetic: 72.1 us -> none  [cell_update(): jax.nn.sigmoid(gate_f) * c_prev + jax.nn.sigmoid(gate_i) * jnp.tanh(gate_g)]
    conv_general_dilated x128 -> x0, local copies, waits for them, and re-layouts: 63 us -> none  [conv_valid(): lax.conv_general_dilated(operand, kernel, (1, 1), 'VALID', dimension_numb...]
    while x322 -> x0, local copies, waits for them, and re-layouts: 62.7 us -> none
    dynamic_update_slice x32 -> x0, local copies, waits for them, and re-layouts: 54.1 us -> none  [local_run(): lax.scan(time_step, (h_init, c_init), frames_ext)]
  transfers between devices with their start and end apart: 132 -> 4, of which waited for: 0 -> 1; matrix products, arithmetic and copies ran while one was open for 19% -> 5% of each run, Pallas kernels for 0% -> 0%
where the time goes in v1:
time: 292 us; the launch traced here: 290 us
  Pallas kernels  196 us (67%)
  local copies, waits for them, and re-layouts  57.7 us (20%)
  other arithmetic  21.9 us (8%)
  starting transfers between devices  11.8 us (4%)
    pallas_call x1, Pallas kernels, local_run(): pl.pallas_call(functools.partial(cell_kernel, cfg), out_shape=(jax.ShapeD...  165 us
    pallas_call x1, Pallas kernels, local_run(): pl.pallas_call(untile_kernel, out_shape=jax.ShapeDtypeStruct((steps, heig...  30.1 us
    slice x2, local copies, waits for them, and re-layouts, local_run(): flat[:, :half + 2]  17.5 us
    slice x1, local copies, waits for them, and re-layouts, local_run(): flat[:, half:]  10.2 us
    another operation x3, other arithmetic, local_run(): jnp.stack([flat[..., dx:dx + width] for dx in range(3)], axis=2)  10.1 us
    ppermute x2, starting transfers between devices, edge_exchange(): from_prev = lax.ppermute(high_part, axis_name, forward)  8.38 us
    concatenate x1, other arithmetic, local_run(): jnp.concatenate([flat[:, :half + 2], flat[:, half:]], axis=3)  6.07 us
  transfers between devices with their start and end apart: 4, of which 1 were waited for; matrix products, arithmetic and copies ran while one was open for 5% of the time, Pallas kernels for 0%

profile of v1, /device:TPU:97, one launch (start us, length us, event | category | flops | bytes accessed | tf_op | source)
XLA Modules:
  0.0 289.9 jit_solution(1292577277073255598)
XLA Ops:
  0.6 3.0 %copy.42 = bf16[32,1,64,64,4]{2,3,4,0,1:T(8,128)(2,1)S(1)} copy(bf16[32,1,64,64,4]{3,4,2,1,0:T(4,128)(2,1)} %param.7) | data formatting | bytes 2097152 | tf_op args[0]
  3.6 3.0 %fusion.9 = (bf16[32,1,4,64]{1,3,2,0:T(8,128)(2,1)}, bf16[32,1,4,64]{1,3,2,0:T(8,128)(2,1)}) fusion(bf16[32,64,4,64]{1,3,2,0:T(8,128)(2,1)S(1)} %bitcast.48), kind=kLoop, calls=%fused_computation.48 | loop fusion | bytes 65536 | tf_op jit(solution)/shard_map/slice | solution.py:283
  6.6 2.2 copy.43
  8.8 4.6 %collective-permute-start = (bf16[32,1,4,64]{3,0,2,1:T(8,128)(2,1)S(1)}, bf16[32,1,4,64]{3,0,2,1:T(8,128)(2,1)S(1)}, u32[]{:S(2)}, u32[]{:S(2)}) collective-permute-start(bf16[32,1,4,64]{3,0,2,1:T(8,128)(2,1)S(1)} %copy.43), channel_id=1, source_target_pairs={{0,1},{1,2},{2,3},{3,4},{4,5},{5,6},{6,7},{8,9},{9,10},{10,11},{11... | collective-permute-start | bytes 49160 | tf_op jit(solution)/shard_map/ppermute | solution.py:289
  13.4 2.7 copy.44
  16.1 1.9 collective-permute-start.1
  18.7 0.1 fusion.2
  19.0 0.2 copy.52
  19.2 0.1 copy.53
  19.4 0.1 maximum_bitcast_fusion.w_ref
  19.6 2.9 %copy.55 = f32[2,32,64,64]{2,0,3,1:T(2,128)S(1)} copy(f32[2,32,64,64]{3,2,1,0:T(8,128)} %bitcast.57) | data formatting | bytes 2097152 | tf_op jit(solution)/shard_map/reshape;squeeze | solution.py:310
  22.6 1.1 reshape.226.c0_ref
  23.7 2.5 copy.54
  26.2 0.5 reshape.225.h0_ref
  26.7 2.0 copy.45
  28.6 2.6 copy.46
  31.3 4.9 %pad_maximum_fusion.8 = bf16[32,66,4,64]{1,3,2,0:T(8,128)(2,1)S(1)} fusion(bf16[32,1,4,64]{1,3,2,0:T(8,128)(2,1)} %copy.46, bf16[32,64,4,64]{1,3,2,0:T(8,128)(2,1)} %bitcast.49, bf16[32,1,4,64]{1,3,2,0:T(8,128)(2,1)} %copy.45), kind=kLoop, calls=%fused_computation.12 | loop fusion | flops 3244032 | bytes 2162688 | tf_op jit(solution)/shard_map/concatenate | solution.py:291
  36.2 0.1 fusion.8
  36.3 3.8 %collective-permute-start.2 = (bf16[32,66,4,1]{1,3,2,0:T(2,128)(2,1)S(1)}, bf16[32,66,4,1]{1,3,2,0:T(2,128)(2,1)S(1)}, u32[]{:S(2)}, u32[]{:S(2)}) collective-permute-start(bf16[32,66,4,1]{1,3,2,0:T(2,128)(2,1)S(1)} %get-tuple-element.21), channel_id=1, source_target_pairs={{0,8},{8,16},{16,24},{1,9},{9,17},{17,25},{2,10},{10,18},{18,26},{... | collective-permute-start | bytes 50696 | tf_op jit(solution)/shard_map/ppermute | solution.py:289
  40.1 1.5 collective-permute-start.3
  41.6 2.0 fusion.10
  43.6 1.9 collective-permute-done.3
  45.5 6.6 %fusion.1 = (bf16[32,66,1,4,64]{1,4,3,2,0:T(8,128)(2,1)S(1)}, bf16[32,66,1,4,64]{1,4,3,2,0:T(8,128)(2,1)S(1)}) fusion(bf16[32,66,4,1]{1,3,2,0:T(2,128)(2,1)S(1)} %collective-permute-done.2, bf16[32,1,4,64]{1,3,2,0:T(8,128)(2,1)S(1)} %copy-done.3, bf16[32,64,4,64]{1,3,2,0:T(8,128)(2,1)S(1)} %bitcast.51, bf16[32,1,4,64]{1,3,2,0:T(8,128)(2,1)S(1)} %copy-done.2, ...), kind=kLoop, calls=%fused_computation.9 | loop fusion | flops 8650752 | bytes 3277824 | tf_op jit(solution)/shard_map/stack | solution.py:316
  52.1 1.6 pad_maximum_fusion
  53.8 7.3 %pad_slice_fusion.1 = (bf16[32,34,16,64]{1,3,2,0:T(8,128)(2,1)}, bf16[32,34,16,64]{1,3,2,0:T(8,128)(2,1)}) fusion(bf16[32,66,12,64]{1,3,2,0:T(8,128)(2,1)S(1)} %bitcast.53), kind=kLoop, calls=%fused_computation.1 | loop fusion | bytes 7700480 | tf_op jit(solution)/shard_map/slice | solution.py:318
  61.0 10.2 %copy.49 = bf16[32,34,16,64]{3,2,1,0:T(8,128)(2,1)} copy(bf16[32,34,16,64]{1,3,2,0:T(8,128)(2,1)} %get-tuple-element.17) | data formatting | bytes 4456448 | tf_op jit(solution)/shard_map/slice | solution.py:318
  71.3 10.2 %copy.50 = bf16[32,34,16,64]{3,2,1,0:T(8,128)(2,1)} copy(bf16[32,34,16,64]{1,3,2,0:T(8,128)(2,1)} %get-tuple-element.18) | data formatting | bytes 4456448 | tf_op jit(solution)/shard_map/slice | solution.py:318
  81.4 6.1 %pad_maximum_fusion.1 = bf16[32,34,16,128]{3,2,1,0:T(8,128)(2,1)S(1)} fusion(bf16[32,34,16,64]{3,2,1,0:T(8,128)(2,1)} %copy.50, bf16[32,34,16,64]{3,2,1,0:T(8,128)(2,1)} %copy.49), kind=kLoop, calls=%fused_computation.3 | loop fusion | flops 8912896 | bytes 8912896 | tf_op jit(solution)/shard_map/concatenate | solution.py:318
  87.6 165.5 %shard_map.86 = (bf16[32,2048,128]{2,1,0:T(8,128)(2,1)}, f32[2048,128]{1,0:T(8,128)S(1)}) custom-call(bf16[32,544,128]{2,1,0:T(8,128)(2,1)S(1)} %bitcast.47, bf16[256,624]{1,0:T(8,128)(2,1)S(1)} %maximum_bitcast_fusion.w_ref, f32[256,128]{1,0:T(8,128)S(1)} %broadcast_in_dim.16.bias_ref, bf16[2048,128]{1,0:T(8,128)(2,1)S(1)} %reshape.225.h0_ref, ...), custom_call_target="tpu_custom_call" | custom-call | tf_op jit(solution)/shard_map/pallas_call | solution.py:330
  253.1 30.1 %shard_map.87 = bf16[32,64,64,64]{3,2,1,0:T(8,128)(2,1)} custom-call(bf16[32,2048,128]{2,1,0:T(8,128)(2,1)} %get-tuple-element.4.x_ref), custom_call_target="tpu_custom_call" | custom-call | tf_op jit(solution)/shard_map/pallas_call | solution.py:345
  283.3 2.5 reshape.227
  285.8 4.1 %copy.56 = f32[2,32,64,64]{3,2,1,0:T(8,128)} copy(f32[2,32,64,64]{2,0,3,1:T(2,128)} %bitcast.54) | data formatting | bytes 2097152 | tf_op jit(solution)/shard_map/transpose | solution.py:352
  (43 shorter events, 1.1 us)
Async XLA Ops:
  3.6 3.0 %copy-start = (bf16[32,1,64,64,4]{2,3,4,0,1:T(8,128)(2,1)}, bf16[32,1,64,64,4]{2,3,4,0,1:T(8,128)(2,1)S(1)}, u32[]{:S(2)}) copy-start(bf16[32,1,64,64,4]{2,3,4,0,1:T(8,128)(2,1)S(1)} %copy.42) | copy-start | bytes 3145732
  6.6 11.5 %copy-start.7 = (s32[4]{0:T(128)S(1)}, s32[4]{0:T(128)}, u32[]{:S(2)}) copy-start(s32[4]{0:T(128)} %constant.67.clone) | copy-start | bytes 52
  6.6 12.4 %copy-start.4 = (bf16[3,3,64,256]{3,2,1,0:T(8,128)(2,1)S(1)}, bf16[3,3,64,256]{3,2,1,0:T(8,128)(2,1)}, u32[]{:S(2)}) copy-start(bf16[3,3,64,256]{3,2,1,0:T(8,128)(2,1)} %param.9) | copy-start | bytes 884740
  6.6 12.6 %copy-start.5 = (bf16[3,3,4,256]{3,2,1,0:T(4,128)(2,1)S(1)}, bf16[3,3,4,256]{3,2,1,0:T(4,128)(2,1)}, u32[]{:S(2)}) copy-start(bf16[3,3,4,256]{3,2,1,0:T(4,128)(2,1)} %param.8) | copy-start | bytes 55300
  8.8 17.9 %collective-permute-start = (bf16[32,1,4,64]{3,0,2,1:T(8,128)(2,1)S(1)}, bf16[32,1,4,64]{3,0,2,1:T(8,128)(2,1)S(1)}, u32[]{:S(2)}, u32[]{:S(2)}) collective-permute-start(bf16[32,1,4,64]{3,0,2,1:T(8,128)(2,1)S(1)} %copy.43), channel_id=1, source_target_pairs={{0,1},{1,2},{2,3},{3,4},{4,5},{5,6},{6,7},{8,9},{9,10},{10,11},{11... | collective-permute-start | bytes 49160 | tf_op jit(solution)/shard_map/ppermute | solution.py:289
  16.1 12.5 %collective-permute-start.1 = (bf16[32,1,4,64]{3,0,2,1:T(8,128)(2,1)}, bf16[32,1,4,64]{3,0,2,1:T(8,128)(2,1)}, u32[]{:S(2)}, u32[]{:S(2)}) collective-permute-start(bf16[32,1,4,64]{3,0,2,1:T(8,128)(2,1)} %copy.44), channel_id=1, source_target_pairs={{1,0},{2,1},{3,2},{4,3},{5,4},{6,5},{7,6},{9,8},{10,9},{11,10},{12... | collective-permute-start | bytes 49160 | tf_op jit(solution)/shard_map/ppermute | solution.py:290
  31.3 10.3 %copy-start.1 = (bf16[32,1,64,64,4]{2,3,4,0,1:T(8,128)(2,1)S(1)}, bf16[32,1,64,64,4]{2,3,4,0,1:T(8,128)(2,1)}, u32[]{:S(2)}) copy-start(bf16[32,1,64,64,4]{2,3,4,0,1:T(8,128)(2,1)} %copy-done) | copy-start | bytes 3145732
  31.3 10.3 %copy-start.2 = (bf16[32,1,4,64]{1,3,2,0:T(8,128)(2,1)S(1)}, bf16[32,1,4,64]{1,3,2,0:T(8,128)(2,1)}, u32[]{:S(2)}) copy-start(bf16[32,1,4,64]{1,3,2,0:T(8,128)(2,1)} %copy.45) | copy-start | bytes 49156
  31.3 10.3 %copy-start.3 = (bf16[32,1,4,64]{1,3,2,0:T(8,128)(2,1)S(1)}, bf16[32,1,4,64]{1,3,2,0:T(8,128)(2,1)}, u32[]{:S(2)}) copy-start(bf16[32,1,4,64]{1,3,2,0:T(8,128)(2,1)} %copy.46) | copy-start | bytes 49156
  36.3 7.3 %collective-permute-start.2 = (bf16[32,66,4,1]{1,3,2,0:T(2,128)(2,1)S(1)}, bf16[32,66,4,1]{1,3,2,0:T(2,128)(2,1)S(1)}, u32[]{:S(2)}, u32[]{:S(2)}) collective-permute-start(bf16[32,66,4,1]{1,3,2,0:T(2,128)(2,1)S(1)} %get-tuple-element.21), channel_id=1, source_target_pairs={{0,8},{8,16},{16,24},{1,9},{9,17},{17,25},{2,10},{10,18},{18,26},{... | collective-permute-start | bytes 50696 | tf_op jit(solution)/shard_map/ppermute | solution.py:289
  40.1 5.4 %collective-permute-start.3 = (bf16[32,66,4,1]{1,3,2,0:T(2,128)(2,1)S(1)}, bf16[32,66,4,1]{1,3,2,0:T(2,128)(2,1)S(1)}, u32[]{:S(2)}, u32[]{:S(2)}) collective-permute-start(bf16[32,66,4,1]{1,3,2,0:T(2,128)(2,1)S(1)} %get-tuple-element.22), channel_id=1, source_target_pairs={{8,0},{16,8},{24,16},{9,1},{17,9},{25,17},{10,2},{18,10},{26,18},{... | collective-permute-start | bytes 50696 | tf_op jit(solution)/shard_map/ppermute | solution.py:290
  81.4 6.1 %copy-start.6 = (f32[256]{0:T(256)S(1)}, f32[256]{0:T(256)}, u32[]{:S(2)}) copy-start(f32[256]{0:T(256)} %param.10) | copy-start | bytes 3076

commit v2 on v1

v2 whole, which is shorter than its diff:
```python
import functools

import jax
import jax.numpy as jnp
import numpy as np
from jax import lax
from jax.experimental import pallas as pl
from jax.experimental.pallas import tpu as pltpu
from jax.sharding import PartitionSpec as P

MESH = pl.DeviceIdType.MESH
BF16, F32 = jnp.bfloat16, jnp.float32
LANES = 128


def chunk_order(n):
    order = [0]
    low, high = 1, n - 1
    while low <= high:
        order.append(low)
        if high != low:
            order.append(high)
        low, high = low + 1, high - 1
    return order


def cell_kernel(cfg, fr_ref, w_ref, bias_ref, h0_ref, c0_ref, mask_ref, out_ref, c_out_ref,
                ha, hb, left_a, left_b, right_a, right_b, gates, c_ref, f_mid, f_left, f_right,
                f_col_out, f_col_in, f_row_out, f_row_in, f_diag_in, f_ssem, f_rsem,
                pieces, col_out, col_in, row_out, row_in, diag_in,
                col_ssem, col_rsem, row_ssem, row_rsem, diag_ssem, diag_rsem, out_sem):
    steps, half, chan, n_chunks, n_rows, n_cols = cfg
    per = half // n_chunks
    groups = chan // 16
    order = chunk_order(n_chunks)
    first, last = 0, n_chunks - 1
    slots = per * groups
    sizes = [size for group in GROUPS for size in group]
    ends = [sum(sizes[:i + 1]) for i in range(len(sizes))]
    home = {chunk: next(card for card, end in enumerate(ends) if place < end) for place, chunk in enumerate(order)}
    base = {chunk: slots * (place - ends[home[chunk]] + sizes[home[chunk]]) for place, chunk in enumerate(order)}
    members = [[chunk for chunk in order if home[chunk] == card] for card in range(len(sizes))]
    card_from = [sum(len(group) for group in GROUPS[:i]) for i in range(len(GROUPS) + 1)]
    group_of = {chunk: max(g for g in range(len(GROUPS)) if card_from[g] <= home[chunk]) for chunk in order}
    closing = {[chunk for chunk in order if group_of[chunk] == g][-1]: g for g in range(len(GROUPS))}
    assert sum(sizes) == n_chunks and max(sizes) * slots <= 32 and home[first] == home[last] == 0
    my_row, my_col = lax.axis_index("rows"), lax.axis_index("cols")
    has_up, has_down = my_row > 0, my_row < n_rows - 1
    has_left, has_right = my_col > 0, my_col < n_cols - 1
    h_refs, l_refs, r_refs = (ha, hb), (left_a, left_b), (right_a, right_b)

    def mask(index):
        return mask_ref[index] > 0

    even, low_half = mask(0), mask(1)
    lane_first, lane_last = mask(2), mask(3)
    second = mask(4)
    bits = [mask(5 + level) for level in range(5)]

    def copy(src, dst, ssem, rsem, drow, dcol):
        return pltpu.make_async_remote_copy(src_ref=src, dst_ref=dst, send_sem=ssem, recv_sem=rsem,
                                            device_id={"rows": my_row + drow, "cols": my_col + dcol}, device_id_type=MESH)

    def col_copy(par, side, group):
        cards = pl.ds(card_from[group], len(GROUPS[group]))
        return copy(col_out.at[par, side, cards], col_in.at[par, side, cards], col_ssem.at[par, side, group],
                    col_rsem.at[par, side, group], 0, 1 if side == 0 else -1)

    def row_copy(par, side):
        return copy(row_out.at[par, side], row_in.at[par, side], row_ssem.at[par, side], row_rsem.at[par, side],
                    1 if side == 0 else -1, 0)

    def diag_copy(par, slot):
        return copy(col_out.at[par, slot % 2, 0], diag_in.at[par, slot], diag_ssem.at[par, slot],
                    diag_rsem.at[par, slot], 1 if slot < 2 else -1, 1 if slot % 2 == 0 else -1)

    col_to, col_from = (has_right, has_left), (has_left, has_right)
    row_to, row_from = (has_down, has_up), (has_up, has_down)
    diag_to = tuple((has_down if s < 2 else has_up) & col_to[s % 2] for s in range(4))
    diag_from = tuple((has_up if s < 2 else has_down) & col_from[s % 2] for s in range(4))

    def when(condition, transfers, method):
        @pl.when(condition)
        def _():
            for transfer in transfers:
                getattr(transfer, method)()

    def each_sent(par, group, condition, method):
        for side in range(2):
            when(col_to[side] & condition, [col_copy(par, side, group)], method)
        if group == 0:
            for side in range(2):
                when(row_to[side] & condition, [row_copy(par, side)], method)
            for slot in range(4):
                when(diag_to[slot] & condition, [diag_copy(par, slot)], method)

    def wait_for(par, group):
        for side in range(2):
            when(col_from[side], [col_copy(par, side, group)], "wait_recv")
        if group == 0:
            for side in range(2):
                when(row_from[side], [row_copy(par, side)], "wait_recv")
            for slot in range(4):
                when(diag_from[slot], [diag_copy(par, slot)], "wait_recv")

    def join(vectors, level):
        while len(vectors) > 1:
            pairs = [vectors[i:i + 2] for i in range(0, len(vectors), 2)]
            vectors = [jnp.where(bits[level], *pair) if len(pair) == 2 else pair[0] for pair in pairs]
            level += 1
        return vectors[0]

    def pack(parts, start):
        quads = [join([parts[i]] + [pltpu.roll(parts[i + j], 2 * j, 1) for j in range(1, 4)], 0) for i in range(0, len(parts), 4)]
        return [join([pltpu.roll(quad, (shift_by + 2 * start + 8 * i) % LANES, 1) for i, quad in enumerate(quads)], 2)
                for shift_by in (65, 63)]

    def shift(cells, message, amount):
        halo = pltpu.roll(message, amount % LANES, 1)
        return (jnp.where(lane_first, halo, pltpu.roll(cells, 1, 1)), jnp.where(lane_last, halo, pltpu.roll(cells, LANES - 1, 1)))

    def shifted(par, row, message, rolls):
        for g in range(groups):
            place = pl.ds(row * chan + 16 * g, 16)
            l_refs[par][place, :], r_refs[par][place, :] = shift(h_refs[par][place, :], message, rolls[g])

    def col_message(par, group):
        return jnp.where(even, col_in[par, 0, group], col_in[par, 1, group])

    def patch(par, chunks, edge):
        for chunk in chunks:
            message = col_message(par, home[chunk])
            for q in range(per):
                shifted(par, chunk * per + q + 1, message, [-2 * (base[chunk] + q * groups + g) for g in range(groups)])
        if edge is not None:
            side = 0 if edge == first else 1
            diag = jnp.where(even, diag_in[par, 2 * side], diag_in[par, 2 * side + 1])
            beside = col_message(par, 0)
            start = base[last] + (per - 1) * groups if edge == first else base[first]
            row = 0 if edge == first else half + 1
            for g in range(groups):
                place = slice(16 * g, 16 * (g + 1))
                mine, theirs = row_out[par, side, place, :], row_in[par, side, place, :]
                joined = jnp.where(low_half, theirs, mine) if edge == first else jnp.where(low_half, mine, theirs)
                h_refs[par][pl.ds(row * chan + 16 * g, 16), :] = joined
            message = jnp.where(second, diag, beside) if edge == first else jnp.where(second, beside, diag)
            shifted(par, row, message, [64 - 2 * (start + g) for g in range(groups)])

    def publish(par, chunk):
        parts = [h_refs[par][pl.ds((chunk * per + s // groups + 1) * chan + 16 * (s % groups), 16), :] for s in range(slots)]
        packed = pack(parts, base[chunk])
        card = home[chunk]
        for side in range(2):
            if chunk == members[card][-1]:
                earlier = [pieces[side, other] for other in members[card][:-1]]
                col_out[par, side, card] = join(earlier + [packed[side]], slots.bit_length() - 1)
            else:
                pieces[side, chunk] = packed[side]
        if chunk in (first, last):
            side = 0 if chunk == last else 1
            row = half if chunk == last else 1
            for g in range(groups):
                row_out[par, side, 16 * g:16 * (g + 1), :] = pltpu.roll(h_refs[par][pl.ds(row * chan + 16 * g, 16), :], 64, 1)

    frame_groups = fr_ref.shape[0]

    def frame_copies():
        for side in range(2):
            yield col_to[side], col_from[side], copy(f_col_out.at[side], f_col_in.at[side], f_ssem.at[side], f_rsem.at[side],
                                                     0, 1 if side == 0 else -1)
        for side in range(2):
            yield row_to[side], row_from[side], copy(f_row_out.at[side], f_row_in.at[side], f_ssem.at[2 + side],
                                                     f_rsem.at[2 + side], 1 if side == 0 else -1, 0)
        for slot in range(4):
            yield diag_to[slot], diag_from[slot], copy(f_col_out.at[slot % 2], f_diag_in.at[slot], f_ssem.at[4 + slot],
                                                       f_rsem.at[4 + slot], 1 if slot < 2 else -1, 1 if slot % 2 == 0 else -1)

    def send_frames():
        def build(tg, carry):
            f_mid[tg, 16:16 * (half + 1), :] = fr_ref[tg]
            f_col_out[0, tg], f_col_out[1, tg] = pack([fr_ref[tg, 16 * k:16 * (k + 1), :] for k in range(half)], 0)
            f_row_out[0, tg] = pltpu.roll(fr_ref[tg, 16 * (half - 1):16 * half, :], 64, 1)
            f_row_out[1, tg] = pltpu.roll(fr_ref[tg, 0:16, :], 64, 1)
            return carry

        lax.fori_loop(0, frame_groups, build, 0)
        for to, _, transfer in frame_copies():
            pl.when(to)(transfer.start)

    def receive_frames():
        for _, source, transfer in frame_copies():
            pl.when(source)(transfer.wait_recv)

        def place(tg, carry):
            message = jnp.where(even, f_col_in[0, tg], f_col_in[1, tg])
            above = jnp.where(even, f_diag_in[0, tg], f_diag_in[1, tg])
            below = jnp.where(even, f_diag_in[2, tg], f_diag_in[3, tg])
            rows = [(0, jnp.where(low_half, f_row_in[0, tg], f_row_out[0, tg]), jnp.where(second, above, message), 64 - 2 * (half - 1))]
            rows += [(k + 1, fr_ref[tg, 16 * k:16 * (k + 1), :], message, -2 * k) for k in range(half)]
            rows += [(half + 1, jnp.where(low_half, f_row_out[1, tg], f_row_in[1, tg]), jnp.where(second, message, below), 64)]
            for row, cells, beside, amount in rows:
                there = slice(16 * row, 16 * (row + 1))
                if row in (0, half + 1):
                    f_mid[tg, there, :] = cells
                f_left[tg, there, :], f_right[tg, there, :] = shift(cells, beside, amount)
            return carry

        lax.fori_loop(0, frame_groups, place, 0)
        for to, _, transfer in frame_copies():
            pl.when(to)(transfer.wait_send)

    def multiply(par, t, chunk, slot):
        blocks = []
        for q in range(per):
            place = pl.ds((chunk * per + q) * chan, 3 * chan)
            there = pl.ds((chunk * per + q) * 16, 48)
            frame = [f[lax.div(t, 4), there, :] for f in (f_left, f_mid, f_right)]
            blocks.append(jnp.concatenate([l_refs[par][place, :], h_refs[par][place, :], r_refs[par][place, :]] + frame, axis=0))
        gates[slot] = jnp.dot(w_ref[lax.rem(t, 4)], jnp.concatenate(blocks, axis=1), preferred_element_type=F32)

    def sigmoid(x):
        return 0.5 * jnp.tanh(0.5 * x) + 0.5

    def update(par, chunk, slot):
        for q in range(per):
            pre = [gates[slot, pl.ds(b * chan, chan), q * LANES:(q + 1) * LANES] + bias_ref[pl.ds(b * chan, chan), :]
                   for b in range(4)]
            place = pl.ds((chunk * per + q) * chan, chan)
            c_next = sigmoid(pre[1]) * c_ref[place, :] + sigmoid(pre[0]) * jnp.tanh(pre[3])
            c_ref[place, :] = c_next
            h_refs[par][pl.ds((chunk * per + q + 1) * chan, chan), :] = (sigmoid(pre[2]) * jnp.tanh(c_next)).astype(BF16)

    def out_copy(par, t):
        return pltpu.make_async_copy(h_refs[par].at[pl.ds(chan, half * chan), :], out_ref.at[t], out_sem.at[par])

    needs, seen = [], set()
    for chunk in order:
        chunks, edge = [], None
        for near in (chunk - 1, chunk, chunk + 1):
            if 0 <= near < n_chunks and near not in seen:
                seen.add(near)
                chunks.append(near)
        if chunk in (first, last):
            edge = chunk
        needs.append((chunks, edge))
    waits, waited = [], set()
    for chunks, edge in needs:
        which = {group_of[chunk] for chunk in chunks} | ({0} if edge is not None else set())
        waits.append(sorted(which - waited))
        waited |= which

    for par in range(2):
        col_in[par] = jnp.zeros(col_in.shape[1:], BF16)
        row_in[par] = jnp.zeros(row_in.shape[1:], BF16)
        diag_in[par] = jnp.zeros(diag_in.shape[1:], BF16)
    for ref in (f_col_in, f_row_in, f_diag_in):
        ref[...] = jnp.zeros(ref.shape, BF16)
    barrier = pltpu.get_barrier_semaphore()
    count = jnp.int32(0)
    for drow in (-1, 0, 1):
        for dcol in (-1, 0, 1):
            if (drow, dcol) == (0, 0):
                continue
            there = jnp.bool_(True)
            if drow:
                there = there & (has_down if drow > 0 else has_up)
            if dcol:
                there = there & (has_right if dcol > 0 else has_left)

            @pl.when(there)
            def _():
                pl.semaphore_signal(barrier, inc=1, device_id={"rows": my_row + drow, "cols": my_col + dcol}, device_id_type=MESH)
            count = count + there.astype(jnp.int32)
    pl.semaphore_wait(barrier, count)

    send_frames()
    for chunk in order:
        for k in range(chunk * per, (chunk + 1) * per):
            ha[pl.ds((k + 1) * chan, chan), :] = jnp.concatenate([h0_ref[k], h0_ref[k + half]], axis=0).T
        publish(0, chunk)
        if chunk in closing:
            each_sent(0, closing[chunk], True, "start")
    for k in range(half):
        c_ref[pl.ds(k * chan, chan), :] = jnp.concatenate([c0_ref[k], c0_ref[k + half]], axis=0).T
    receive_frames()

    def step(t, par, old):
        live = t < steps - 1

        @pl.when(old)
        def _():
            out_copy(1 - par, t - 2).wait()
        for group in range(len(GROUPS)):
            each_sent(1 - par, group, t > 0, "wait_send")
        for group in waits[0]:
            wait_for(par, group)
        patch(par, *needs[0])

        def finish(i):
            chunk = order[i]
            update(1 - par, chunk, i % 2)
            publish(1 - par, chunk)
            if chunk in closing:
                each_sent(1 - par, closing[chunk], live, "start")

        for i, chunk in enumerate(order):
            if i + 1 < n_chunks:
                for group in waits[i + 1]:
                    wait_for(par, group)
            multiply(par, t, chunk, i % 2)
            if i + 1 < n_chunks:
                patch(par, *needs[i + 1])
            if i > 0:
                finish(i - 1)
        finish(n_chunks - 1)
        out_copy(1 - par, t).start()

    def two_steps(i, carry):
        step(2 * i, 0, i > 0)
        step(2 * i + 1, 1, i > 0)
        return carry

    lax.fori_loop(0, steps // 2, two_steps, 0)
    for group in range(len(GROUPS)):
        each_sent(1, group, True, "wait_send")
    for k in range(half):
        cells = c_ref[pl.ds(k * chan, chan), :].T
        c_out_ref[k], c_out_ref[k + half] = cells[:LANES // 2], cells[LANES // 2:]
    out_copy(1, steps - 2).wait()
    out_copy(0, steps - 1).wait()


def lane_masks():
    lane = np.arange(LANES)
    even, slot = lane % 2 == 0, (lane + 1) // 2 % 32
    second = np.where(even, lane >= 64, (lane < 62) | (lane == 127))
    rows = [even, lane < 64, lane % 64 == 0, lane % 64 == 63, second] + [(slot >> level) % 2 == 0 for level in range(5)]
    return jnp.asarray(np.broadcast_to(np.stack(rows)[:, None, :], (len(rows), 16, LANES)).astype(np.float32), BF16)


def untile_kernel(x_ref, o_ref):
    half, chan = o_ref.shape[1] // 2, o_ref.shape[3]
    for t in range(o_ref.shape[0]):
        for k in range(half):
            cells = x_ref[t, pl.ds(k * chan, chan), :].T
            o_ref[t, k] = cells[:LANES // 2]
            o_ref[t, k + half] = cells[LANES // 2:]


N_CHUNKS = 16
GROUPS = ((3, 3, 3), (4, 3))
UNTILE = 4


def solution(mesh):
    n_rows, n_cols = mesh.shape["rows"], mesh.shape["cols"]
    seq_spec = P(None, "dp", "rows", "cols", None)
    state_spec = P("dp", "rows", "cols", None)

    def local_run(frames, w_in, w_rec, gate_bias, h_init, c_init):
        steps, batch, height, width, c_in = frames.shape
        chan = h_init.shape[-1]
        half = height // 2
        assert batch == 1 and width == 64 and chan == 64 and c_in == 4 and steps % 2 == 0
        assert steps % 4 == 0 and half == 32
        per = half // N_CHUNKS
        gates_n = w_rec.shape[-1]
        parts = frames.reshape(steps // 4, 4, 2, half, width, c_in).transpose(0, 3, 1, 5, 2, 4)
        parts = parts.reshape(steps // 4, half * 16, LANES)
        pick = jnp.eye(4, dtype=BF16)[:, None, None, :, None, None]
        w_x = (pick * w_in.transpose(1, 0, 2, 3)[None, :, :, None]).reshape(4, 9 * 16, gates_n)
        w_h = jnp.broadcast_to(w_rec.transpose(1, 0, 2, 3).reshape(1, 9 * chan, gates_n), (4, 9 * chan, gates_n))
        weights = jnp.concatenate([w_h, w_x], axis=1).transpose(0, 2, 1)
        bias = jnp.broadcast_to(gate_bias[:, None], (gates_n, LANES))

        vmem = pl.BlockSpec(memory_space=pltpu.VMEM)
        cells = pltpu.VMEM(((half + 2) * chan, LANES), BF16)
        dma = pltpu.SemaphoreType.DMA
        cards = sum(len(group) for group in GROUPS)
        cfg = (steps, half, chan, N_CHUNKS, n_rows, n_cols)
        hidden, c_last = pl.pallas_call(
            functools.partial(cell_kernel, cfg),
            out_shape=(jax.ShapeDtypeStruct((steps, half * chan, LANES), BF16), jax.ShapeDtypeStruct((height, width, chan), F32)),
            in_specs=[vmem] * 6,
            out_specs=(pl.BlockSpec(memory_space=pl.ANY), vmem),
            scratch_shapes=[cells] * 6 + [
                pltpu.VMEM((2, gates_n, per * LANES), F32), pltpu.VMEM((half * chan, LANES), F32),
            ] + [pltpu.VMEM((steps // 4, (half + 2) * 16, LANES), BF16)] * 3 + [
                pltpu.VMEM((2, steps // 4, 16, LANES), BF16), pltpu.VMEM((2, steps // 4, 16, LANES), BF16),
                pltpu.VMEM((2, steps // 4, 16, LANES), BF16), pltpu.VMEM((2, steps // 4, 16, LANES), BF16),
                pltpu.VMEM((4, steps // 4, 16, LANES), BF16), dma((8,)), dma((8,)),
                pltpu.VMEM((2, N_CHUNKS, 16, LANES), BF16),
                pltpu.VMEM((2, 2, cards, 16, LANES), BF16), pltpu.VMEM((2, 2, cards, 16, LANES), BF16),
                pltpu.VMEM((2, 2, chan, LANES), BF16), pltpu.VMEM((2, 2, chan, LANES), BF16),
                pltpu.VMEM((2, 4, 16, LANES), BF16),
                dma((2, 2, len(GROUPS))), dma((2, 2, len(GROUPS))), dma((2, 2)), dma((2, 2)), dma((2, 4)), dma((2, 4)), dma((2,)),
            ],
            compiler_params=pltpu.CompilerParams(collective_id=0, has_side_effects=True, vmem_limit_bytes=40 * 1024 * 1024),
        )(parts, weights, bias, h_init[0], c_init[0], lane_masks())

        hidden_seq = pl.pallas_call(
            untile_kernel,
            out_shape=jax.ShapeDtypeStruct((steps, height, width, chan), BF16),
            grid=(steps // UNTILE,),
            in_specs=[pl.BlockSpec((UNTILE, half * chan, LANES), lambda t: (t, 0, 0))],
            out_specs=pl.BlockSpec((UNTILE, height, width, chan), lambda t: (t, 0, 0, 0)),
        )(hidden)
        return hidden_seq[:, None], c_last[None]

    return jax.shard_map(local_run, mesh=mesh, in_specs=(seq_spec, P(), P(), P(), state_spec, state_spec),
                         out_specs=(seq_spec, state_spec), check_vma=False)
```

time: 292 us -> 203 us (0.70)
  local copies, waits for them, and re-layouts: 57.7 us -> 18.3 us
  other arithmetic: 21.9 us -> 0.39 us
  Pallas kernels: 196 us -> 183 us
  starting transfers between devices: 11.8 us -> 0 us
    slice x7 -> x0, local copies, waits for them, and re-layouts: 35.7 us -> none  [the longest x2 17.5 us: local_run(): flat[:, :half + 2]]
    ppermute x4 -> x0, starting transfers between devices: 11.8 us -> none  [the longest x2 8.38 us: edge_exchange(): from_prev = lax.ppermute(high_part, axis_name, forward)]
    concatenate x4 -> x0, other arithmetic: 11.1 us -> none  [the longest x1 6.07 us: local_run(): jnp.concatenate([flat[:, :half + 2], flat[:, half:]], axis=3)]
    another operation x3 -> x0, other arithmetic: 10.1 us -> none  [local_run(): jnp.stack([flat[..., dx:dx + width] for dx in range(3)], axis=2)]
    pallas_call x1, Pallas kernels: 30.1 us -> 20.3 us  [local_run(): pl.pallas_call(untile_kernel, out_shape=jax.ShapeDtypeStruct((steps, heig...]
    another operation x3 -> x0, local copies, waits for them, and re-layouts: 5.46 us -> none  [the longest x2 5.4 us: to_lanes(): parts = state[0].reshape(2, half, width, chan).transpose(1, 3, 0, 2)]
    unnamed x18 -> x14, local copies, waits for them, and re-layouts: 3.03 us -> 7.67 us
    ppermute x2 -> x0, local copies, waits for them, and re-layouts: 4.6 us -> none  [the longest x1 2.65 us: edge_exchange(): from_next = lax.ppermute(low_part, axis_name, backward)]
  transfers between devices with their start and end apart: 4 -> 0, of which waited for: 1 -> 0; matrix products, arithmetic and copies ran while one was open for 5% -> 0% of each run, Pallas kernels for 0% -> 0%
where the time goes in v2:
time: 203 us
  Pallas kernels  183 us (90%)
  local copies, waits for them, and re-layouts  18.3 us (9%)
    pallas_call x1, Pallas kernels, local_run(): pl.pallas_call(functools.partial(cell_kernel, cfg), out_shape=(jax.ShapeD...  163 us
    pallas_call x1, Pallas kernels, local_run(): pl.pallas_call(untile_kernel, out_shape=jax.ShapeDtypeStruct((steps, heig...  20.3 us
    unnamed x14, local copies, waits for them, and re-layouts  7.67 us
    reshape x1, local copies, waits for them, and re-layouts, local_run(): frames.reshape(steps // 4, 4, 2, half, width, c_in)  4.56 us

profile of v2, /device:TPU:97, one launch (start us, length us, event | category | flops | bytes accessed | tf_op | source)
XLA Modules:
  0.0 202.8 jit_solution(10366684367433440741)
XLA Ops:
  0.6 0.7 copy.15
  1.4 0.1 mul.22
  1.5 0.1 mul.23
  1.6 0.1 copy.16
  1.7 0.8 broadcast_in_dim.23.bias_ref
  2.5 1.0 copy.13
  3.5 0.2 copy.14
  3.8 0.1 broadcast_in_dim.22
  3.9 0.0 copy-start.5
  3.9 0.3 maximum_bitcast_fusion.w_ref
  4.2 1.2 copy-done.5
  5.5 4.6 %copy.19 = bf16[8,4,2,32,64,4]{4,2,5,1,3,0:T(2,128)(2,1)} copy(bf16[8,4,2,32,64,4]{4,5,3,2,1,0:T(4,128)(2,1)S(1)} %bitcast.21) | data formatting | bytes 2097152 | tf_op jit(solution)/shard_map/reshape | solution.py:368
  10.0 0.0 copy-start.4
  10.0 3.9 %reshape.26.fr_ref = bf16[8,512,128]{2,1,0:T(8,128)(2,1)S(1)} reshape(bf16[8,32,4,4,2,64]{5,4,3,2,1,0:T(2,128)(2,1)} %bitcast.20) | data formatting | bytes 2097152 | tf_op jit(solution)/shard_map/reshape | solution.py:369
  13.9 0.0 copy-done.4
  13.9 0.0 copy-start
  13.9 1.6 copy-done
  15.5 0.0 copy-start.3
  15.5 1.2 copy-done.3
  16.7 163.2 %shard_map.86 = (bf16[32,2048,128]{2,1,0:T(8,128)(2,1)}, f32[64,64,64]{2,1,0:T(8,128)S(1)}) custom-call(bf16[8,512,128]{2,1,0:T(8,128)(2,1)S(1)} %reshape.26.fr_ref, bf16[4,256,720]{2,1,0:T(8,128)(2,1)S(1)} %maximum_bitcast_fusion.w_ref, f32[256,128]{1,0:T(8,128)S(1)} %broadcast_in_dim.23.bias_ref, bf16[64,64,64]{2,1,0:T(8,128)(2,1)S(1)} %bitcast.18, ...), custom_call_target="tpu_custom_call" | custom-call | tf_op jit(solution)/shard_map/pallas_call | solution.py:381
  179.9 0.0 copy-start.1
  179.9 1.3 copy-done.1
  181.2 0.0 copy-start.2
  181.2 20.3 %shard_map.87 = bf16[32,64,64,64]{3,2,1,0:T(8,128)(2,1)} custom-call(bf16[32,2048,128]{2,1,0:T(8,128)(2,1)} %get-tuple-element.4.x_ref), custom_call_target="tpu_custom_call" | custom-call | tf_op jit(solution)/shard_map/pallas_call | solution.py:401
  201.5 0.0 copy-done.2
  201.5 1.3 copy.21
  (4 shorter events, 0.1 us)
Async XLA Ops:
  3.9 1.6 copy-start.5
  10.0 3.9 %copy-start.4 = (bf16[10,16,128]{2,1,0:T(8,128)(2,1)S(1)}, bf16[10,16,128]{2,1,0:T(8,128)(2,1)}, u32[]{:S(2)}) copy-start(bf16[10,16,128]{2,1,0:T(8,128)(2,1)} %constant.2.clone.mask_ref) | copy-start | bytes 122884
  13.9 1.6 copy-start
  15.5 1.2 copy-start.3
  179.9 1.3 copy-start.1
  181.2 20.3 %copy-start.2 = (f32[64,64,64]{2,1,0:T(8,128)S(1)}, f32[64,64,64]{2,1,0:T(8,128)}, u32[]{:S(2)}) copy-start(f32[64,64,64]{2,1,0:T(8,128)} %copy-done.1) | copy-start | bytes 3145732

commit v3 on v2

--- a/solution.py
+++ b/solution.py
@@ -21,7 +21,7 @@
         if high != low:
             order.append(high)
         low, high = low + 1, high - 1
-    return order
+    return [(chunk + n // 2) % n for chunk in order]
 
 
 def cell_kernel(cfg, fr_ref, w_ref, bias_ref, h0_ref, c0_ref, mask_ref, out_ref, c_out_ref,
@@ -43,7 +43,7 @@
     card_from = [sum(len(group) for group in GROUPS[:i]) for i in range(len(GROUPS) + 1)]
     group_of = {chunk: max(g for g in range(len(GROUPS)) if card_from[g] <= home[chunk]) for chunk in order}
     closing = {[chunk for chunk in order if group_of[chunk] == g][-1]: g for g in range(len(GROUPS))}
-    assert sum(sizes) == n_chunks and max(sizes) * slots <= 32 and home[first] == home[last] == 0
+    assert sum(sizes) == n_chunks and max(sizes) * slots <= 32 and home[first] == home[last]
     my_row, my_col = lax.axis_index("rows"), lax.axis_index("cols")
     has_up, has_down = my_row > 0, my_row < n_rows - 1
     has_left, has_right = my_col > 0, my_col < n_cols - 1
@@ -66,12 +66,14 @@
         return copy(col_out.at[par, side, cards], col_in.at[par, side, cards], col_ssem.at[par, side, group],
                     col_rsem.at[par, side, group], 0, 1 if side == 0 else -1)
 
+    edge_card, edge_group = home[first], group_of[first]
+
     def row_copy(par, side):
         return copy(row_out.at[par, side], row_in.at[par, side], row_ssem.at[par, side], row_rsem.at[par, side],
                     1 if side == 0 else -1, 0)
 
     def diag_copy(par, slot):
-        return copy(col_out.at[par, slot % 2, 0], diag_in.at[par, slot], diag_ssem.at[par, slot],
+        return copy(col_out.at[par, slot % 2, edge_card], diag_in.at[par, slot], diag_ssem.at[par, slot],
                     diag_rsem.at[par, slot], 1 if slot < 2 else -1, 1 if slot % 2 == 0 else -1)
 
     col_to, col_from = (has_right, has_left), (has_left, has_right)
@@ -88,7 +90,7 @@
     def each_sent(par, group, condition, method):
         for side in range(2):
             when(col_to[side] & condition, [col_copy(par, side, group)], method)
-        if group == 0:
+        if group == edge_group:
             for side in range(2):
                 when(row_to[side] & condition, [row_copy(par, side)], method)
             for slot in range(4):
@@ -97,11 +99,12 @@
     def wait_for(par, group):
         for side in range(2):
             when(col_from[side], [col_copy(par, side, group)], "wait_recv")
-        if group == 0:
-            for side in range(2):
-                when(row_from[side], [row_copy(par, side)], "wait_recv")
-            for slot in range(4):
-                when(diag_from[slot], [diag_copy(par, slot)], "wait_recv")
+
+    def wait_edges(par):
+        for side in range(2):
+            when(row_from[side], [row_copy(par, side)], "wait_recv")
+        for slot in range(4):
+            when(diag_from[slot], [diag_copy(par, slot)], "wait_recv")
 
     def join(vectors, level):
         while len(vectors) > 1:
@@ -135,7 +138,7 @@
         if edge is not None:
             side = 0 if edge == first else 1
             diag = jnp.where(even, diag_in[par, 2 * side], diag_in[par, 2 * side + 1])
-            beside = col_message(par, 0)
+            beside = col_message(par, edge_card)
             start = base[last] + (per - 1) * groups if edge == first else base[first]
             row = 0 if edge == first else half + 1
             for g in range(groups):
@@ -245,7 +248,7 @@
         needs.append((chunks, edge))
     waits, waited = [], set()
     for chunks, edge in needs:
-        which = {group_of[chunk] for chunk in chunks} | ({0} if edge is not None else set())
+        which = {group_of[chunk] for chunk in chunks} | ({edge_group} if edge is not None else set())
         waits.append(sorted(which - waited))
         waited |= which
 
@@ -302,6 +305,8 @@
             publish(1 - par, chunk)
             if chunk in closing:
                 each_sent(1 - par, closing[chunk], live, "start")
+                if closing[chunk] == 0:
+                    wait_edges(par)
 
         for i, chunk in enumerate(order):
             if i + 1 < n_chunks:
@@ -348,7 +353,7 @@
 
 
 N_CHUNKS = 16
-GROUPS = ((3, 3, 3), (4, 3))
+GROUPS = ((3, 3, 3), (3, 4))
 UNTILE = 4
 
 

time: 203 us -> 198 us (0.975)
  Pallas kernels: 183 us -> 178 us
    pallas_call x1, Pallas kernels: 163 us -> 158 us  [local_run(): pl.pallas_call(functools.partial(cell_kernel, cfg), out_shape=(jax.ShapeD...]
where the time goes in v3:
time: 198 us
  Pallas kernels  178 us (90%)
  local copies, waits for them, and re-layouts  18.3 us (9%)
    pallas_call x1, Pallas kernels, local_run(): pl.pallas_call(functools.partial(cell_kernel, cfg), out_shape=(jax.ShapeD...  158 us
    pallas_call x1, Pallas kernels, local_run(): pl.pallas_call(untile_kernel, out_shape=jax.ShapeDtypeStruct((steps, heig...  20.3 us
    unnamed x14, local copies, waits for them, and re-layouts  7.67 us
    reshape x1, local copies, waits for them, and re-layouts, local_run(): frames.reshape(steps // 4, 4, 2, half, width, c_in)  4.56 us

profile of v3, /device:TPU:97, one launch (start us, length us, event | category | flops | bytes accessed | tf_op | source)
XLA Modules:
  0.0 197.6 jit_solution(6502752540240269377)
XLA Ops:
  0.6 0.7 copy.15
  1.4 0.1 mul.22
  1.5 0.1 mul.23
  1.6 0.1 copy.16
  1.7 0.8 broadcast_in_dim.23.bias_ref
  2.5 1.0 copy.13
  3.5 0.2 copy.14
  3.8 0.1 broadcast_in_dim.22
  3.9 0.0 copy-start.5
  3.9 0.3 maximum_bitcast_fusion.w_ref
  4.2 1.2 copy-done.5
  5.5 4.6 %copy.19 = bf16[8,4,2,32,64,4]{4,2,5,1,3,0:T(2,128)(2,1)} copy(bf16[8,4,2,32,64,4]{4,5,3,2,1,0:T(4,128)(2,1)S(1)} %bitcast.21) | data formatting | bytes 2097152 | tf_op jit(solution)/shard_map/reshape | solution.py:373
  10.0 0.0 copy-start.4
  10.0 3.9 %reshape.26.fr_ref = bf16[8,512,128]{2,1,0:T(8,128)(2,1)S(1)} reshape(bf16[8,32,4,4,2,64]{5,4,3,2,1,0:T(2,128)(2,1)} %bitcast.20) | data formatting | bytes 2097152 | tf_op jit(solution)/shard_map/reshape | solution.py:374
  13.9 0.0 copy-done.4
  13.9 0.0 copy-start
  13.9 1.6 copy-done
  15.5 0.0 copy-start.3
  15.5 1.2 copy-done.3
  16.7 158.0 %shard_map.86 = (bf16[32,2048,128]{2,1,0:T(8,128)(2,1)}, f32[64,64,64]{2,1,0:T(8,128)S(1)}) custom-call(bf16[8,512,128]{2,1,0:T(8,128)(2,1)S(1)} %reshape.26.fr_ref, bf16[4,256,720]{2,1,0:T(8,128)(2,1)S(1)} %maximum_bitcast_fusion.w_ref, f32[256,128]{1,0:T(8,128)S(1)} %broadcast_in_dim.23.bias_ref, bf16[64,64,64]{2,1,0:T(8,128)(2,1)S(1)} %bitcast.18, ...), custom_call_target="tpu_custom_call" | custom-call | tf_op jit(solution)/shard_map/pallas_call | solution.py:386
  174.7 0.0 copy-start.1
  174.8 1.3 copy-done.1
  176.1 0.0 copy-start.2
  176.1 20.3 %shard_map.87 = bf16[32,64,64,64]{3,2,1,0:T(8,128)(2,1)} custom-call(bf16[32,2048,128]{2,1,0:T(8,128)(2,1)} %get-tuple-element.4.x_ref), custom_call_target="tpu_custom_call" | custom-call | tf_op jit(solution)/shard_map/pallas_call | solution.py:406
  196.3 0.0 copy-done.2
  196.3 1.3 copy.21
  (4 shorter events, 0.1 us)
Async XLA Ops:
  3.9 1.6 copy-start.5
  10.0 3.9 %copy-start.4 = (bf16[10,16,128]{2,1,0:T(8,128)(2,1)S(1)}, bf16[10,16,128]{2,1,0:T(8,128)(2,1)}, u32[]{:S(2)}) copy-start(bf16[10,16,128]{2,1,0:T(8,128)(2,1)} %constant.2.clone.mask_ref) | copy-start | bytes 122884
  13.9 1.6 copy-start
  15.5 1.2 copy-start.3
  174.7 1.3 copy-start.1
  176.1 20.3 %copy-start.2 = (f32[64,64,64]{2,1,0:T(8,128)S(1)}, f32[64,64,64]{2,1,0:T(8,128)}, u32[]{:S(2)}) copy-start(f32[64,64,64]{2,1,0:T(8,128)} %copy-done.1) | copy-start | bytes 3145732
